TPU v7x, 32 devices: a whole 2x2x4 slice. The times are simulated.
32 devices in a mesh: seq: 8 (over z, y), head: 4 (over x, core).
Axes of the slice: x: 2, y: 2, z: 4, core: 2. Of those that a mesh axis runs over, the one named last changes fastest.
Arguments:
- tokens: bfloat16 [4096, 2048], P('seq'), may hold values from -100 to 100
- seq_ids: int32 [4096], P('seq'), may hold values from 0 to 15, never falling along the last dimension, each value on 1 to 1024 neighbouring positions
- w_query: bfloat16 [2048, 3072], P(None, 'head'), may hold values from -0.125 to 0.125
- w_down: bfloat16 [2048, 576], replicated, may hold values from -0.125 to 0.125
- latent_gain: float32 [512], replicated, may hold values from 0.1 to 1.9
- w_key_up: bfloat16 [16, 128, 512], P('head'), may hold values from -0.5 to 0.5
- w_value_up: bfloat16 [16, 512, 128], P('head'), may hold values from -0.25 to 0.25
- w_out: bfloat16 [2048, 2048], P('head'), may hold values from -0.125 to 0.125
Outputs:
- attended: bfloat16 [4096, 2048], P('seq', 'head')
Inputs may be any that keep to these rules, and one draw needn't show every extreme that they name: `seq_ids`: prompt numbers never fall along the tokens; each of the 16 prompts holds 1 to 1024 tokens, one exactly 1024.
All inputs are finite; a program needn't handle non-finite values.
Results may differ from a plain program's by a relative error of at most 0.014.
Values may be sent and summed in bfloat16 or wider, within the bound.
A program may use at most 128 MiB of HBM per device.

v0:
```python
import jax
import jax.numpy as jnp
from jax import lax
from jax.sharding import PartitionSpec as P

epsilon = 1e-06
far_below = -1e30


def shifted(block, axis, distance):
    devices = range(lax.axis_size(axis))
    route = [(i - distance, i) for i in devices if i - distance in devices]
    return lax.ppermute(block, axis, route)


def rotate(values, positions):
    half_width = values.shape[-1] // 2
    inverse = 10000.0 ** (-2.0 * jnp.arange(half_width, dtype=jnp.float32) / values.shape[-1])
    angles = positions.astype(jnp.float32)[:, None] * inverse[None, :]
    padding_dims = (1,) * (values.ndim - 2)
    cosine = jnp.cos(angles).reshape(angles.shape[:1] + padding_dims + angles.shape[1:])
    sine_table = jnp.sin(angles).reshape(angles.shape[:1] + padding_dims + angles.shape[1:])
    low_half = values[..., :half_width]
    high_half = values[..., half_width:]
    return jnp.concatenate(
        [low_half * cosine - high_half * sine_table, high_half * cosine + low_half * sine_table],
        axis=-1,
    )


def local(tokens, seq_ids, w_query, w_down, latent_gain, w_key_up, w_value_up, w_out):
    tok_rows = tokens.shape[0]
    local_heads = w_key_up.shape[0]
    nope_width = w_key_up.shape[1]
    latent_width = w_key_up.shape[2]
    rope_width = w_down.shape[1] - latent_width
    seq_devices = lax.axis_size("seq")
    first_row = lax.axis_index("seq") * tok_rows
    row_index = jnp.arange(tok_rows, dtype=jnp.int32)
    starts = jnp.concatenate([jnp.ones((1,), jnp.bool_), seq_ids[1:] != seq_ids[:-1]])
    local_begin = lax.cummax(jnp.where(starts, row_index, 0), axis=0) + first_row
    last_seg = seq_ids[tok_rows - 1 :]
    last_begin = local_begin[tok_rows - 1 :]
    all_segs, all_begins = (
        lax.all_gather(last_seg, "seq", axis=0, tiled=True),
        lax.all_gather(last_begin, "seq", axis=0, tiled=True),
    )
    earlier_mask = jnp.arange(seq_devices, dtype=jnp.int32) < lax.axis_index("seq")
    carried_seg = jnp.max(jnp.where(earlier_mask, all_segs, -1))
    carried_begin = jnp.min(
        jnp.where(earlier_mask & (all_segs == carried_seg), all_begins, first_row)
    )
    positions = (
        first_row + row_index - jnp.where(seq_ids == carried_seg, carried_begin, local_begin)
    )
    query = jnp.dot(tokens, w_query, preferred_element_type=jnp.float32).astype(jnp.bfloat16)
    query = query.reshape(tok_rows, local_heads, nope_width + rope_width)
    down = jnp.dot(tokens, w_down, preferred_element_type=jnp.float32)
    latent_raw = down[:, :latent_width]
    latent = (
        latent_raw
        * lax.rsqrt(jnp.mean(latent_raw * latent_raw, axis=1, keepdims=True) + epsilon)
        * latent_gain
    ).astype(jnp.bfloat16)
    key_rope = rotate(down[:, latent_width:], positions).astype(jnp.bfloat16)
    query_rope = rotate(query[:, :, nope_width:].astype(jnp.float32), positions).astype(
        jnp.bfloat16
    )
    query_latent = jnp.einsum(
        "thn,hnc->htc", query[:, :, :nope_width], w_key_up, preferred_element_type=jnp.float32
    ).astype(jnp.bfloat16)
    query_flat = jnp.concatenate([query_latent, query_rope.transpose(1, 0, 2)], axis=2)
    query_flat = query_flat.reshape(local_heads * tok_rows, latent_width + rope_width)
    key_block = jnp.concatenate([latent, key_rope], axis=1)
    key_tags = seq_ids.astype(jnp.bfloat16)
    query_index = first_row + row_index
    score_scale = (nope_width + rope_width) ** (-0.5)

    def attend_part(running, key_rows, key_marks, key_first):
        key_count = key_rows.shape[0]
        key_segs = key_marks.astype(jnp.int32)
        key_index = key_first + jnp.arange(key_count, dtype=jnp.int32)
        top_old, total_old, sum_old = running
        scores = (
            lax.dot_general(
                query_flat, key_rows, (((1,), (1,)), ((), ())), preferred_element_type=jnp.float32
            )
            * score_scale
        )
        allowed = (
            (key_segs[None, :] == seq_ids[:, None])
            & (key_index[None, :] <= query_index[:, None])
            & (key_index[None, :] >= 0)
        )
        allowed = jnp.tile(allowed, (local_heads, 1))
        top_new = jnp.maximum(top_old, jnp.max(jnp.where(allowed, scores, far_below), axis=1))
        weights = jnp.where(allowed, jnp.exp(scores - top_new[:, None]), 0.0)
        rescale = jnp.exp(top_old - top_new)
        total_new = total_old * rescale + jnp.sum(weights, axis=1)
        sum_new = sum_old * rescale[:, None] + jnp.dot(
            weights.astype(jnp.bfloat16),
            key_rows[:, :latent_width],
            preferred_element_type=jnp.float32,
        )
        return (top_new, total_new, sum_new)

    flat_rows = local_heads * tok_rows
    initial = (
        jnp.full((flat_rows,), far_below, jnp.float32),
        jnp.zeros((flat_rows,), jnp.float32),
        jnp.zeros((flat_rows, latent_width), jnp.float32),
    )
    running = attend_part(initial, key_block, key_tags, first_row)
    passed = (key_block, key_tags)
    for distance in range(1, seq_devices // 4 + 1):
        passed = shifted((passed[0], passed[1]), "seq", 1)
        running = attend_part(running, passed[0], passed[1], first_row - distance * tok_rows)
    top_final, total_final, sum_final = running
    latent_out = (
        (sum_final / total_final[:, None])
        .astype(jnp.bfloat16)
        .reshape(local_heads, tok_rows, latent_width)
    )
    head_out = jnp.einsum(
        "htc,hcv->thv", latent_out, w_value_up, preferred_element_type=jnp.float32
    ).astype(jnp.bfloat16)
    head_out = head_out.reshape(tok_rows, local_heads * w_value_up.shape[2])
    partial_out = jnp.dot(head_out, w_out, preferred_element_type=jnp.float32)
    return lax.psum_scatter(
        partial_out.astype(jnp.bfloat16), "head", scatter_dimension=1, tiled=True
    )


def solution(mesh):
    return jax.shard_map(
        local,
        mesh=mesh,
        in_specs=(
            P("seq", None),
            P("seq"),
            P(None, "head"),
            P(),
            P(),
            P("head", None, None),
            P("head", None, None),
            P("head", None),
        ),
        out_specs=P("seq", "head"),
        check_vma=False,
    )
```

profile of v0, /device:TPU:8, one launch (start us, length us, event | category | flops | bytes accessed | tf_op | source)
XLA Modules:
  0.0 124.6 jit_solution(17086968151183858529)
XLA Ops:
  6.5 0.9 slice_compare_fusion
  8.1 1.2 dynamic-slice
  9.3 1.5 %slice_dynamic-update-slice_fusion.1 = s32[8]{0:T(128)S(1)} fusion(s32[8]{0:T(128)S(1)} %broadcast.306.clone.1, u32[]{:T(128)} %bitcast.1, s32[512]{0:T(512)} %param.9), kind=kLoop, calls=%fused_computation.70 | loop fusion | bytes 40
  11.7 10.5 %all-reduce.2 = (s32[8]{0:T(128)S(1)}, s32[8]{0:T(128)S(1)}) all-reduce(s32[8]{0:T(128)S(1)} %slice_dynamic-update-slice_fusion, s32[8]{0:T(128)S(1)} %slice_dynamic-update-slice_fusion.1), channel_id=1, replica_groups=mesh['seq'=8,'head'=4] {'seq'}, use_global_device_ids=true, to_apply=%add.1 | all-reduce | flops 16 | bytes 128
  22.8 1.4 %fusion.28 = s32[]{:T(128)} fusion(s32[8]{0:T(128)S(1)} %get-tuple-element.5, s32[8]{0:T(128)S(1)} %get-tuple-element.6, s32[]{:T(128)S(6)} %mul.136, s32[]{:T(128)} %fusion.27, s32[]{:T(128)S(6)} %axis_index.19), kind=kLoop, calls=%fused_computation.71 | loop fusion | flops 39 | bytes 80 | tf_op jit(solution)/shard_map/reduce_min | solution.py:50
  24.2 2.1 %fusion.39 = (s32[512]{0:T(512)S(1)}, bf16[512]{0:T(512)(128)(2,1)S(1)}, f32[512]{0:T(512)S(1)}) fusion(s32[512]{0:T(512)} %param.9, s32[512]{0:T(512)S(1)} %add_bitcast_fusion, s32[]{:T(128)} %fusion.28, s32[]{:T(128)} %fusion.27, s32[]{:T(128)S(6)} %mul.136), kind=kLoop, calls=%fused_computation.81 | loop fusion | flops 3584 | bytes 9228 | tf_op jit(solution)/shard_map/convert_element_type | solution.py:81
  26.3 3.4 %collective-permute-start = (bf16[512]{0:T(512)(128)(2,1)S(1)}, bf16[512]{0:T(512)(128)(2,1)S(1)}, u32[]{:S(2)}, u32[]{:S(2)}) collective-permute-start(bf16[512]{0:T(512)(128)(2,1)S(1)} %get-tuple-element.13), channel_id=1, source_target_pairs={{0,4},{4,8},{8,12},{12,16},{16,20},{20,24},{24,28},{1,5},{5,9},{9,... | collective-permute-start | bytes 3080 | tf_op jit(solution)/shard_map/ppermute | solution.py:13
  29.7 3.7 %fusion.40 = f32[512,576]{0,1:T(8,128)S(1)} fusion(bf16[512,2048]{1,0:T(8,128)(2,1)} %param.8, bf16[2048,576]{0,1:T(8,128)(2,1)} %param.11), kind=kOutput, calls=%fused_computation.82 | convolution fusion | flops 1207959552 | bytes 5636096 | tf_op jit(solution)/shard_map/dot_general | solution.py:58
  35.7 2.3 %collective-permute-start.1 = (bf16[512,576]{0,1:T(8,128)(2,1)}, bf16[512,576]{0,1:T(8,128)(2,1)}, u32[]{:S(2)}, u32[]{:S(2)}) collective-permute-start(bf16[512,576]{0,1:T(8,128)(2,1)} %pad_maximum_fusion), channel_id=1, source_target_pairs={{0,4},{4,8},{8,12},{12,16},{16,20},{20,24},{24,28},{1,5},{5,9},{9,... | collective-permute-start | bytes 1769480 | tf_op jit(solution)/shard_map/ppermute | solution.py:13
  38.0 4.3 %convolution_convert_fusion.2 = bf16[512,768]{1,0:T(8,128)(2,1)} fusion(bf16[512,2048]{1,0:T(8,128)(2,1)} %param.8, bf16[2048,768]{1,0:T(8,128)(2,1)S(1)} %copy-done), kind=kOutput, calls=%fused_computation.28 | convolution fusion | flops 1611005952 | bytes 6029312 | tf_op jit(solution)/shard_map/dot_general | solution.py:56
  42.3 2.3 %copy.13 = bf16[512,768]{0,1:T(8,128)(2,1)} copy(bf16[512,768]{1,0:T(8,128)(2,1)} %convolution_convert_fusion.2) | data formatting | bytes 1572864 | tf_op jit(solution)/shard_map/convert_element_type | solution.py:56
  44.6 1.0 slice_convert_fusion
  45.6 2.0 %convolution_convert_fusion.1 = bf16[4,512,512]{1,2,0:T(8,128)(2,1)S(1)} fusion(bf16[4,128,512]{2,1,0:T(8,128)(2,1)} %param.13, bf16[512,4,192]{0,2,1:T(8,128)(2,1)} %bitcast.57), kind=kOutput, calls=%fused_computation.27 | convolution fusion | flops 269484032 | bytes 3145728 | tf_op jit(solution)/shard_map/thn,hnc->htc/dot_general | solution.py:69
  47.9 3.4 %collective-permute-start.2 = (bf16[512]{0:T(512)(128)(2,1)S(1)}, bf16[512]{0:T(512)(128)(2,1)S(1)}, u32[]{:S(2)}, u32[]{:S(2)}) collective-permute-start(bf16[512]{0:T(512)(128)(2,1)S(1)} %collective-permute-done), channel_id=1, source_target_pairs={{0,4},{4,8},{8,12},{12,16},{16,20},{20,24},{24,28},{1,5},{5,9},{9,... | collective-permute-start | bytes 3080 | tf_op jit(solution)/shard_map/ppermute | solution.py:13
  51.7 2.5 %collective-permute-done.2 = bf16[512]{0:T(512)(128)(2,1)S(1)} collective-permute-done((bf16[512]{0:T(512)(128)(2,1)S(1)}, bf16[512]{0:T(512)(128)(2,1)S(1)}, u32[]{:S(2)}, u32[]{:S(2)}) %collective-permute-start.2) | collective-permute-done | bytes 1056 | tf_op jit(solution)/shard_map/ppermute | solution.py:13
  54.3 1.1 and_and_fusion.2
  55.4 0.9 tile.12
  57.0 2.7 %collective-permute-start.3 = (bf16[512,576]{0,1:T(8,128)(2,1)}, bf16[512,576]{0,1:T(8,128)(2,1)S(1)}, u32[]{:S(2)}, u32[]{:S(2)}) collective-permute-start(bf16[512,576]{0,1:T(8,128)(2,1)} %collective-permute-done.1), channel_id=1, source_target_pairs={{0,4},{4,8},{8,12},{12,16},{16,20},{20,24},{24,28},{1,5},{5,9},{9,... | collective-permute-start | bytes 1769480 | tf_op jit(solution)/shard_map/ppermute | solution.py:13
  59.7 2.3 %select_reduce_fusion.2 = (f32[2048]{0:T(1024)S(1)}, f32[2048,512]{0,1:T(8,128)S(1)}) fusion(pred[2048,512]{0,1:T(8,128)(4,1)S(1)} %bitcast.47, bf16[2048,576]{0,1:T(8,128)(2,1)S(1)} %bitcast.58, bf16[512,32]{0,1:T(8,128)(2,1)S(1)} %get-tuple-element.15, bf16[512,32]{0,1:T(8,128)(2,1)S(1)} %get-tuple-element.14, bf16[512,512]{0,1:T(8,128)(2,1)S(1)} %copy-done.2), kind=kOutput, calls=%fused_computation.6 | convolution fusion | flops 1212872704 | bytes 8200192 | tf_op jit(solution)/shard_map/dot_general | solution.py:85
  62.0 0.9 tile.31
  63.6 0.9 tile.14
  65.2 3.4 %select_reduce_fusion.1 = (f32[2048]{0:T(1024)S(1)}, f32[2048,512]{0,1:T(8,128)S(1)}) fusion(pred[2048,512]{0,1:T(8,128)(4,1)S(1)} %bitcast.50, bf16[2048,576]{0,1:T(8,128)(2,1)S(1)} %bitcast.59, bf16[512,576]{0,1:T(8,128)(2,1)} %collective-permute-done.1), kind=kOutput, calls=%fused_computation.4 | convolution fusion | flops 1211103232 | bytes 8200192 | tf_op jit(solution)/shard_map/dot_general | solution.py:85
  68.5 2.5 %collective-permute-done.3 = bf16[512,576]{0,1:T(8,128)(2,1)S(1)} collective-permute-done((bf16[512,576]{0,1:T(8,128)(2,1)}, bf16[512,576]{0,1:T(8,128)(2,1)S(1)}, u32[]{:S(2)}, u32[]{:S(2)}) %collective-permute-start.3) | collective-permute-done | bytes 589856 | tf_op jit(solution)/shard_map/ppermute | solution.py:13
  71.0 2.2 %select_reduce_fusion = (f32[2048]{0:T(1024)S(1)}, f32[2048,512]{0,1:T(8,128)S(1)}) fusion(pred[2048,512]{0,1:T(8,128)(4,1)S(1)} %bitcast.44, bf16[2048,576]{0,1:T(8,128)(2,1)S(1)} %bitcast.60, bf16[512,576]{0,1:T(8,128)(2,1)S(1)} %collective-permute-done.3), kind=kOutput, calls=%fused_computation.2 | convolution fusion | flops 1211103232 | bytes 8200192 | tf_op jit(solution)/shard_map/dot_general | solution.py:85
  73.3 1.1 fusion
  74.4 1.5 %fusion.10 = f32[2048,512]{1,0:T(8,128)S(1)} fusion(bf16[512,512]{0,1:T(8,128)(2,1)S(1)} %copy-done.2, pred[2048,512]{0,1:T(8,128)(4,1)S(1)} %bitcast.49, f32[2048,512]{0,1:T(8,128)S(1)} %get-tuple-element.31, f32[2048]{0:T(1024)S(1)} %get-tuple-element.19), kind=kOutput, calls=%fused_computation.17 | convolution fusion | flops 1077936128 | bytes 9969664 | tf_op jit(solution)/shard_map/dot_general | solution.py:100
  75.9 1.3 %fusion.4 = f32[2048]{0:T(1024)S(1)} fusion(pred[2048,512]{0,1:T(8,128)(4,1)S(1)} %bitcast.45, f32[2048,512]{0,1:T(8,128)S(1)} %get-tuple-element.27, f32[2048]{0:T(1024)S(1)} %get-tuple-element.10), kind=kLoop, calls=%fused_computation.12 | loop fusion | flops 4192256 | bytes 5259264 | tf_op jit(solution)/shard_map/reduce_sum | solution.py:99
  77.2 1.1 fusion.2
  78.3 2.5 %fusion.8 = f32[2048,512]{1,0:T(8,128)S(1)} fusion(pred[2048,512]{0,1:T(8,128)(4,1)S(1)} %bitcast.52, f32[2048,512]{0,1:T(8,128)S(1)} %get-tuple-element.29, f32[2048]{0:T(1024)S(1)} %get-tuple-element.11, bf16[512,576]{0,1:T(8,128)(2,1)} %collective-permute-done.1), kind=kOutput, calls=%fused_computation.16 | convolution fusion | flops 1077936128 | bytes 9969664 | tf_op jit(solution)/shard_map/dot_general | solution.py:100
  80.9 3.9 %divide_convert_fusion = bf16[2048,512]{1,0:T(8,128)(2,1)S(1)} fusion(f32[2048,512]{1,0:T(8,128)S(1)} %fusion.8, f32[2048,512]{1,0:T(8,128)S(1)} %fusion.10, f32[2048]{0:T(1024)S(1)} %get-tuple-element.7, f32[2048]{0:T(1024)S(1)} %get-tuple-element.9, f32[2048]{0:T(1024)S(1)} %get-tuple-element.8, f32[2048]{0:T(1024)S(1)} %get-tuple-element.18, ...), kind=kOutput, calls=%fused_computation | convolution fusion | flops 1085276160 | bytes 16293888 | tf_op jit(solution)/shard_map/dot_general | solution.py:100
  85.6 2.6 %convolution_convert_fusion = bf16[512,2048]{1,0:T(8,128)(2,1)} fusion(bf16[512,512]{0,1:T(8,128)(2,1)S(1)} %bitcast.62, bf16[512,2048]{1,0:T(8,128)(2,1)S(1)} %copy-done.6), kind=kOutput, calls=%fused_computation.7 | convolution fusion | flops 1074790400 | bytes 4718592 | tf_op jit(solution)/shard_map/dot_general | solution.py:128
  88.2 29.5 %reduce-scatter.2.cloned.1.call-done = bf16[512,512]{1,0:T(8,128)(2,1)} async-done(((bf16[512,2048]{1,0:T(8,128)(2,1)}), bf16[512,512]{1,0:T(8,128)(2,1)}) %reduce-scatter.2.cloned.1.call-update) | async-done | bytes 524304 | tf_op jit(solution)/shard_map/reduce_scatter | solution.py:129
  (50 shorter events, 7.8 us)
Async XLA Ops:
  6.5 31.5 %copy-start = (bf16[2048,768]{1,0:T(8,128)(2,1)S(1)}, bf16[2048,768]{1,0:T(8,128)(2,1)}, u32[]{:S(2)}) copy-start(bf16[2048,768]{1,0:T(8,128)(2,1)} %param.10) | copy-start | bytes 9437188
  6.5 111.2 %reduce-scatter.2.cloned.1.call-start = ((), (), s32[]{:S(2)}) async-start(), calls=%async_computation.1 | async-start | bytes 2621440 | tf_op jit(solution)/shard_map/reduce_scatter | solution.py:129
  26.3 21.6 %collective-permute-start = (bf16[512]{0:T(512)(128)(2,1)S(1)}, bf16[512]{0:T(512)(128)(2,1)S(1)}, u32[]{:S(2)}, u32[]{:S(2)}) collective-permute-start(bf16[512]{0:T(512)(128)(2,1)S(1)} %get-tuple-element.13), channel_id=1, source_target_pairs={{0,4},{4,8},{8,12},{12,16},{16,20},{20,24},{24,28},{1,5},{5,9},{9,... | collective-permute-start | bytes 3080 | tf_op jit(solution)/shard_map/ppermute | solution.py:13
  29.7 4.2 %copy-start.5 = (f32[512]{0:T(512)S(1)}, f32[512]{0:T(512)}, u32[]{:S(2)}) copy-start(f32[512]{0:T(512)} %param.12) | copy-start | bytes 6148
  34.1 0.8 copy-start.1
  35.7 21.3 %collective-permute-start.1 = (bf16[512,576]{0,1:T(8,128)(2,1)}, bf16[512,576]{0,1:T(8,128)(2,1)}, u32[]{:S(2)}, u32[]{:S(2)}) collective-permute-start(bf16[512,576]{0,1:T(8,128)(2,1)} %pad_maximum_fusion), channel_id=1, source_target_pairs={{0,4},{4,8},{8,12},{12,16},{16,20},{20,24},{24,28},{1,5},{5,9},{9,... | collective-permute-start | bytes 1769480 | tf_op jit(solution)/shard_map/ppermute | solution.py:13
  47.7 6.6 %copy-start.4 = (s32[512]{0:T(512)S(1)}, s32[512]{0:T(512)}, u32[]{:S(2)}) copy-start(s32[512]{0:T(512)} %param.9) | copy-start | bytes 6148
  47.9 6.4 %collective-permute-start.2 = (bf16[512]{0:T(512)(128)(2,1)S(1)}, bf16[512]{0:T(512)(128)(2,1)S(1)}, u32[]{:S(2)}, u32[]{:S(2)}) collective-permute-start(bf16[512]{0:T(512)(128)(2,1)S(1)} %collective-permute-done), channel_id=1, source_target_pairs={{0,4},{4,8},{8,12},{12,16},{16,20},{20,24},{24,28},{1,5},{5,9},{9,... | collective-permute-start | bytes 3080 | tf_op jit(solution)/shard_map/ppermute | solution.py:13
  51.4 8.3 %copy-start.2 = (bf16[512,512]{0,1:T(8,128)(2,1)S(1)}, bf16[512,512]{0,1:T(8,128)(2,1)}, u32[]{:S(2)}) copy-start(bf16[512,512]{0,1:T(8,128)(2,1)} %copy-done.1) | copy-start | bytes 1572868
  57.0 14.0 %collective-permute-start.3 = (bf16[512,576]{0,1:T(8,128)(2,1)}, bf16[512,576]{0,1:T(8,128)(2,1)S(1)}, u32[]{:S(2)}, u32[]{:S(2)}) collective-permute-start(bf16[512,576]{0,1:T(8,128)(2,1)} %collective-permute-done.1), channel_id=1, source_target_pairs={{0,4},{4,8},{8,12},{12,16},{16,20},{20,24},{24,28},{1,5},{5,9},{9,... | collective-permute-start | bytes 1769480 | tf_op jit(solution)/shard_map/ppermute | solution.py:13
  80.8 3.9 %copy-start.3 = (bf16[4,512,128]{2,1,0:T(8,128)(2,1)S(1)}, bf16[4,512,128]{2,1,0:T(8,128)(2,1)}, u32[]{:S(2)}) copy-start(bf16[4,512,128]{2,1,0:T(8,128)(2,1)} %param.14) | copy-start | bytes 1572868
  80.9 4.7 %copy-start.6 = (bf16[512,2048]{1,0:T(8,128)(2,1)S(1)}, bf16[512,2048]{1,0:T(8,128)(2,1)}, u32[]{:S(2)}) copy-start(bf16[512,2048]{1,0:T(8,128)(2,1)} %param.15) | copy-start | bytes 6291460
Sparse Core Ops, SparseCore 0:
  88.4 29.3 reduce-scatter.1
where the time goes:
time: 127 us; the launch traced here: 125 us
  waiting for transfers between devices  34.5 us (27%)
  matrix products  29.1 us (23%)
  between operations  13.8 us (11%)
  other arithmetic  12.9 us (10%)
  local copies, waits for them, and re-layouts  11.9 us (9%)
  starting transfers between devices  11.8 us (9%)
  blocking collectives  10.5 us (8%)
    reduce_scatter x1, waiting for transfers between devices, local(): lax.psum_scatter(partial_out.astype(jnp.bfloat16), 'head', scatter_dimens...  29.5 us
    ppermute x4, starting transfers between devices, shifted(): return lax.ppermute(block, axis, route)  11.8 us
    unnamed x1, blocking collectives  10.5 us
    dot_general x3, matrix products, attend_part(): lax.dot_general(query_flat, key_rows, (((1,), (1,)), ((), ())), preferred...  7.88 us
    dot_general x3, matrix products, attend_part(): jnp.dot(weights.astype(jnp.bfloat16), key_rows[:, :latent_width], preferr...  7.8 us
    unnamed x22, local copies, waits for them, and re-layouts  6.24 us
    ppermute x4, waiting for transfers between devices, shifted(): return lax.ppermute(block, axis, route)  5.03 us
    dot_general x1, matrix products, local(): jnp.dot(tokens, w_query, preferred_element_type=jnp.float32)  4.26 us
  transfers between devices with their start and end apart: 5, of which 3 were waited for; matrix products, arithmetic and copies ran while one was open for 21% of the time, Pallas kernels for 0%

commit v1 on v0

v1 whole, which is shorter than its diff:
```python
import functools
import math

import jax
import jax.numpy as jnp
from jax import lax
from jax.experimental import pallas as pl
from jax.experimental.pallas import tpu as pltpu
from jax.sharding import PartitionSpec as P

MESH = pl.DeviceIdType.MESH
epsilon = 1e-06
far_below = -1e30
PROMPTS = 16
f32 = jnp.float32
bf16 = jnp.bfloat16


def dot(a, b):
    return jnp.dot(a, b, preferred_element_type=f32)


def dot_t(a, b):
    return lax.dot_general(a, b, (((1,), (1,)), ((), ())), preferred_element_type=f32)


def attend_kernel(
    n, reach, tok_hbm, ids_ref, wq_hbm, wd_hbm, gain_ref, wk_hbm, wv_hbm, inv_ref, out_ref,
    tok, wq, wd, wk, wv, ids_r, lat, rop, q_s, k_s, v_s, beg, top, total, acc,
    load, s_id, r_id, s_key, r_key, s_fwd, r_fwd,
):
    rows = tok.shape[0]
    half = rows // 2
    latent_width = lat.shape[2]
    heads, _, value = acc.shape
    rope = inv_ref.shape[0] * 2
    nope = wk.shape[0] // heads
    seq = lax.axis_index("seq")
    head = lax.axis_index("head")
    parity = lax.rem(head, 2)
    mate = head + 1 - 2 * parity

    loads = [
        pltpu.make_async_copy(tok_hbm, tok, load.at[0]),
        pltpu.make_async_copy(wd_hbm, wd, load.at[1]),
        pltpu.make_async_copy(wq_hbm, wq, load.at[2]),
        pltpu.make_async_copy(wk_hbm, wk, load.at[3]),
    ]
    for h in range(heads):
        loads.append(
            pltpu.make_async_copy(
                wv_hbm.at[h], wv.at[:, h * value : (h + 1) * value], load.at[4 + h]
            )
        )
    for copy in loads:
        copy.start()

    barrier = pltpu.get_barrier_semaphore()
    pl.semaphore_signal(barrier, inc=1, device_id=(seq, mate), device_id_type=MESH)
    for d in range(1, reach + 1):

        @pl.when(seq + d < n)
        def _():
            pl.semaphore_signal(barrier, inc=1, device_id=(seq + d, head), device_id_type=MESH)

        @pl.when(seq >= d)
        def _():
            pl.semaphore_signal(barrier, inc=1, device_id=(seq - d, head), device_id_type=MESH)

    pl.semaphore_wait(
        barrier, 1 + jnp.minimum(seq, reach) + jnp.minimum(n - 1 - seq, reach)
    )

    def id_copy(d):
        return pltpu.make_async_remote_copy(
            src_ref=ids_ref, dst_ref=ids_r.at[d - 1], send_sem=s_id.at[d - 1],
            recv_sem=r_id.at[d - 1], device_id=(seq + d, head), device_id_type=MESH,
        )

    lat_rows = pl.ds(pl.multiple_of(parity * half, half), half)
    rop_rows = pl.ds(pl.multiple_of(parity * (half // 2), half // 2), half // 2)

    def key_copies(d):
        return [
            pltpu.make_async_remote_copy(
                src_ref=buf.at[0, part], dst_ref=buf.at[d, part], send_sem=s_key.at[d - 1, i],
                recv_sem=r_key.at[d - 1, i], device_id=(seq + d, head), device_id_type=MESH,
            )
            for i, (buf, part) in enumerate(((lat, lat_rows), (rop, rop_rows)))
        ]

    def forward_copies(d):
        return [
            pltpu.make_async_remote_copy(
                src_ref=buf.at[d, part], dst_ref=buf.at[d, part], send_sem=s_fwd.at[d - 1, i],
                recv_sem=r_fwd.at[d - 1, i], device_id=(seq, mate), device_id_type=MESH,
            )
            for i, (buf, part) in enumerate(((lat, lat_rows), (rop, rop_rows)))
        ]

    for d in range(1, reach + 1):

        @pl.when(seq + d < n)
        def _():
            id_copy(d).start()

        @pl.when(seq < d)
        def _():
            ids_r[d - 1] = jnp.full(ids_r.shape[1:], -1, jnp.int32)
            lat[d] = jnp.zeros(lat.shape[1:], bf16)
            rop[d] = jnp.zeros(rop.shape[1:], bf16)

    loads[0].wait()
    loads[1].wait()
    down = dot(tok[...], wd[...])
    raw = down[:, :latent_width]
    latent = (
        raw * lax.rsqrt(jnp.mean(raw * raw, axis=1, keepdims=True) + epsilon) * gain_ref[...]
    )
    lat[0] = latent.astype(bf16)

    for d in range(1, reach + 1):

        @pl.when(seq >= d)
        def _():
            id_copy(d).wait_recv()

    ids = ids_ref[...]
    marks = lax.broadcasted_iota(jnp.int32, (PROMPTS, rows), 0)
    below = jnp.sum((ids < marks).astype(f32), axis=1, keepdims=True)
    same = jnp.zeros((PROMPTS, 1), f32)
    for d in range(1, reach + 1):
        same = same + jnp.sum((ids_r[d - 1] == marks).astype(f32), axis=1, keepdims=True)
    begin = jnp.sum(jnp.where(ids == marks, below - same, 0.0), axis=0, keepdims=True)
    position = lax.broadcasted_iota(jnp.int32, (1, rows), 1).astype(f32) - begin
    angles = inv_ref[...] * position
    cosine, sine = jnp.cos(angles), jnp.sin(angles)
    cosine = jnp.concatenate([cosine] * (128 // (rope // 2)), axis=0).T[:, :rope]
    sine = jnp.concatenate([-sine, sine] * (128 // rope), axis=0).T[:, :rope]
    beg[...] = jnp.broadcast_to(begin, (128, rows)).T.astype(jnp.int32)

    def rotate(v):
        swapped = jnp.concatenate([v[:, rope // 2 :], v[:, : rope // 2]], axis=1)
        return (v * cosine + swapped * sine).astype(bf16)

    key_rope = rotate(down[:, latent_width:])
    rop[0] = jnp.concatenate([key_rope[:half], key_rope[half:]], axis=1)

    for d in range(1, reach + 1):

        @pl.when(seq + d < n)
        def _():
            for copy in key_copies(d):
                copy.start()

    loads[2].wait()
    query = dot(tok[...], wq[...]).astype(bf16)
    width = nope + rope
    pad = jnp.zeros((rows, q_s.shape[2] - width), bf16)
    for h in range(heads):
        at = h * width
        q_s[h] = jnp.concatenate(
            [
                query[:, at : at + nope],
                rotate(query[:, at + nope : at + width].astype(f32)),
                pad,
            ],
            axis=1,
        )
    for copy in loads[3:]:
        copy.wait()

    scale = (nope + rope) ** (-0.5) * math.log2(math.e)

    def expand(d):
        block = lat[d]
        keys = dot_t(block, wk[...]).astype(bf16)
        v_s[...] = dot(block, wv[...]).astype(bf16)
        packed = rop[d]
        tail = jnp.concatenate([packed[:, :rope], packed[:, rope:]], axis=0)
        tail = jnp.concatenate([tail, pad], axis=1)
        for h in range(heads):
            k_s[h] = jnp.concatenate([keys[:, h * nope : (h + 1) * nope], tail], axis=1)

    def piece(d, part, low, high):
        span = high - low
        q_at = part * half
        key_index = lax.broadcasted_iota(jnp.int32, (half, span), 1) + (low - d * rows)
        allowed = key_index >= beg[q_at : q_at + half, :1]
        if d == 0:
            allowed = allowed & (
                key_index <= lax.broadcasted_iota(jnp.int32, (half, span), 0) + q_at
            )
        for h in range(heads):
            mine = (h, slice(q_at, q_at + half))
            scores = dot_t(q_s[mine], k_s[h, low:high]) * scale
            scores = jnp.where(allowed, scores, far_below)
            best = jnp.max(scores, axis=1, keepdims=True)
            if d > 0:
                old = top[mine][:, :1]
                best = jnp.maximum(old, best)
                shrink = jnp.exp2(old - best)
            weights = jnp.exp2(scores - best)
            sums = jnp.sum(weights, axis=1, keepdims=True)
            mixed = dot(weights.astype(bf16), v_s[low:high, h * value : (h + 1) * value])
            if d > 0:
                sums = sums + total[mine][:, :1] * shrink
                mixed = mixed + acc[mine] * shrink
            if d < reach:
                top[mine] = jnp.broadcast_to(best, (half, 128))
                total[mine] = jnp.broadcast_to(sums, (half, 128))
                acc[mine] = mixed
            else:
                out_ref[q_at : q_at + half, h * value : (h + 1) * value] = (mixed / sums).astype(
                    bf16
                )

    expand(0)
    piece(0, 0, 0, half)
    piece(0, 1, 0, rows)
    for d in range(1, reach + 1):

        @pl.when(seq >= d)
        def _():
            for copy, forward in zip(key_copies(d), forward_copies(d)):
                copy.wait_recv()
                forward.start()

    for d in range(1, reach + 1):

        @pl.when(seq >= d)
        def _():
            for forward in forward_copies(d):
                forward.wait_recv()

        expand(d)
        piece(d, 0, 0, rows)
        piece(d, 1, half if d == reach else 0, rows)

    for d in range(1, reach + 1):

        @pl.when(seq + d < n)
        def _():
            id_copy(d).wait_send()
            for copy in key_copies(d):
                copy.wait_send()

        @pl.when(seq >= d)
        def _():
            for forward in forward_copies(d):
                forward.wait_send()


def scatter_kernel(
    chunks, ho_ref, w_hbm, out_ref, w, far_out, far_in, own_out, own_in, x_out, x_in,
    load, s_far, r_far, s_own, r_own, s_x, r_x,
):
    seq = lax.axis_index("seq")
    head = lax.axis_index("head")
    columns = out_ref.shape[1]
    depth = out_ref.shape[0] // chunks
    mate = head + 1 - 2 * lax.rem(head, 2)
    across = lax.rem(head + 2, 4)
    far = lax.rem(mate + 2, 4)
    loads = []
    for i, target in enumerate((far, across, mate, head)):
        part = pl.ds(pl.multiple_of(target * columns, columns), columns)
        loads.append(pltpu.make_async_copy(w_hbm.at[:, part], w.at[i], load.at[i]))
        loads[i].start()
    barrier = pltpu.get_barrier_semaphore()
    for other in (mate, across):
        pl.semaphore_signal(barrier, inc=1, device_id=(seq, other), device_id_type=MESH)
    pl.semaphore_wait(barrier, 2)

    def send(src, dst, c, s, r, other):
        return pltpu.make_async_remote_copy(
            src_ref=src.at[c], dst_ref=dst.at[c], send_sem=s.at[c], recv_sem=r.at[c],
            device_id=(seq, other), device_id_type=MESH,
        )

    def partial(c, i):
        return dot(ho_ref[c * depth : (c + 1) * depth], w[i])

    to_far = [send(far_out, far_in, c, s_far, r_far, mate) for c in range(chunks)]
    to_own = [send(own_out, own_in, c, s_own, r_own, mate) for c in range(chunks)]
    to_x = [send(x_out, x_in, c, s_x, r_x, across) for c in range(chunks)]
    loads[0].wait()
    for c in range(chunks):
        far_out[c] = partial(c, 0).astype(bf16)
        to_far[c].start()
    loads[1].wait()
    for c in range(chunks):
        mine = partial(c, 1)
        to_far[c].wait_recv()
        x_out[c] = (mine + far_in[c].astype(f32)).astype(bf16)
        to_x[c].start()
    loads[2].wait()
    for c in range(chunks):
        own_out[c] = partial(c, 2).astype(bf16)
        to_own[c].start()
    loads[3].wait()
    for c in range(chunks):
        mine = partial(c, 3)
        to_own[c].wait_recv()
        mine = mine + own_in[c].astype(f32)
        to_x[c].wait_recv()
        out_ref[c * depth : (c + 1) * depth] = (mine + x_in[c].astype(f32)).astype(bf16)
    for copy in to_far + to_own + to_x:
        copy.wait_send()


def local(tokens, seq_ids, w_query, w_down, latent_gain, w_key_up, w_value_up, w_out):
    rows, width = tokens.shape
    heads, nope, latent_width = w_key_up.shape
    value = w_value_up.shape[2]
    rope = w_down.shape[1] - latent_width
    n = lax.axis_size("seq")
    groups = lax.axis_size("head")
    reach = max(1, n // 4)
    padded = -(-(nope + rope) // 128) * 128
    inverse = 10000.0 ** (-2.0 * jnp.arange(rope // 2, dtype=f32) / rope)
    vmem = pl.BlockSpec(memory_space=pltpu.VMEM)
    anywhere = pl.BlockSpec(memory_space=pl.ANY)
    dma = pltpu.SemaphoreType.DMA
    head_out = pl.pallas_call(
        functools.partial(attend_kernel, n, reach),
        out_shape=jax.ShapeDtypeStruct((rows, heads * value), bf16),
        in_specs=[anywhere, vmem, anywhere, anywhere, vmem, anywhere, anywhere, vmem],
        out_specs=vmem,
        scratch_shapes=[
            pltpu.VMEM((rows, width), bf16),
            pltpu.VMEM(w_query.shape, bf16),
            pltpu.VMEM(w_down.shape, bf16),
            pltpu.VMEM((heads * nope, latent_width), bf16),
            pltpu.VMEM((latent_width, heads * value), bf16),
            pltpu.VMEM((reach, 1, rows), jnp.int32),
            pltpu.VMEM((reach + 1, rows, latent_width), bf16),
            pltpu.VMEM((reach + 1, rows // 2, 2 * rope), bf16),
            pltpu.VMEM((heads, rows, padded), bf16),
            pltpu.VMEM((heads, rows, padded), bf16),
            pltpu.VMEM((rows, heads * value), bf16),
            pltpu.VMEM((rows, 128), jnp.int32),
            pltpu.VMEM((heads, rows, 128), f32),
            pltpu.VMEM((heads, rows, 128), f32),
            pltpu.VMEM((heads, rows, value), f32),
            dma((4 + heads,)),
            dma((reach,)),
            dma((reach,)),
            dma((reach, 2)),
            dma((reach, 2)),
            dma((reach, 2)),
            dma((reach, 2)),
        ],
        compiler_params=pltpu.CompilerParams(
            collective_id=0, has_side_effects=True, vmem_limit_bytes=56 * 1024 * 1024
        ),
        name="attend",
    )(
        tokens,
        seq_ids.reshape(1, rows),
        w_query,
        w_down,
        latent_gain.reshape(1, latent_width),
        w_key_up.reshape(heads * nope, latent_width),
        w_value_up,
        inverse.reshape(rope // 2, 1),
    )
    columns = w_out.shape[1] // groups
    if groups != 4:
        partial = dot(head_out, w_out).astype(bf16)
        return lax.psum_scatter(partial, "head", scatter_dimension=1, tiled=True)
    chunks = 4
    block = (chunks, rows // chunks, columns)
    return pl.pallas_call(
        functools.partial(scatter_kernel, chunks),
        out_shape=jax.ShapeDtypeStruct((rows, columns), bf16),
        in_specs=[vmem, anywhere],
        out_specs=vmem,
        scratch_shapes=[pltpu.VMEM((4, w_out.shape[0], columns), bf16)]
        + [pltpu.VMEM(block, bf16)] * 6
        + [dma((4,))]
        + [dma((chunks,))] * 6,
        compiler_params=pltpu.CompilerParams(
            collective_id=1, has_side_effects=True, vmem_limit_bytes=32 * 1024 * 1024
        ),
        name="scatter",
    )(head_out, w_out)


def solution(mesh):
    return jax.shard_map(
        local,
        mesh=mesh,
        in_specs=(
            P("seq", None),
            P("seq"),
            P(None, "head"),
            P(),
            P(),
            P("head", None, None),
            P("head", None, None),
            P("head", None),
        ),
        out_specs=P("seq", "head"),
        check_vma=False,
    )
```

time: 127 us -> 54.6 us (0.43)
  the two profiles are of different devices: /device:TPU:8 before, /device:TPU:23 now
where the time goes in v1:
time: 54.6 us; the launch traced here: 54.3 us
  Pallas kernels  47.5 us (87%)
  local copies, waits for them, and re-layouts  6.16 us (11%)
  other arithmetic  0.62 us (1%)
    pallas_call x1, Pallas kernels, local(): pl.pallas_call(functools.partial(attend_kernel, n, reach), out_shape=jax....  30.2 us
    pallas_call x1, Pallas kernels, local(): pl.pallas_call(functools.partial(scatter_kernel, chunks), out_shape=jax.S...  17.3 us
    unnamed x6, local copies, waits for them, and re-layouts  6.16 us

profile of v1, /device:TPU:23, one launch (start us, length us, event | category | flops | bytes accessed | tf_op | source)
XLA Modules:
  0.0 54.3 jit_solution(5196128541713334031)
XLA Ops:
  0.0 0.6 %multiply_power_fusion.inv_ref = f32[32,1]{1,0:T(8,128)} fusion(), kind=kLoop, calls=%fused_computation | loop fusion | flops 32 | bytes 128 | tf_op jit(solution)/shard_map/pow | solution.py:321
  0.6 4.3 %copy.9.wd_hbm = bf16[2048,576]{1,0:T(8,128)(2,1)} copy(bf16[2048,576]{0,1:T(8,128)(2,1)} %param.11) | data formatting | bytes 4718592 | tf_op args[3]
  5.0 0.0 copy-start
  5.0 30.2 %attend.1.ho_ref = bf16[512,512]{1,0:T(8,128)(2,1)} custom-call(bf16[512,2048]{1,0:T(8,128)(2,1)} %tok_hbm.1, s32[1,512]{1,0:T(1,128)} %bitcast.4, bf16[2048,768]{1,0:T(8,128)(2,1)} %wq_hbm.1, bf16[2048,576]{1,0:T(8,128)(2,1)} %copy.9.wd_hbm, f32[1,512]{1,0:T(1,128)} %bitcast.5, bf16[512,512]{1,0:T(8,128)(2,1)} %bitcast.3, bf16[4,512,128]{2,1,0:T(8,128)(2,1)} %wv_hbm.1, ...), custom_call_target="tpu_custom_call" | custom-call | tf_op jit(solution)/shard_map/attend/pallas_call | solution.py:325
  35.1 0.0 copy-done
  35.2 0.0 copy-start.1
  35.2 1.0 %copy-done.1 = bf16[512,512]{1,0:T(8,128)(2,1)S(1)} copy-done((bf16[512,512]{1,0:T(8,128)(2,1)S(1)}, bf16[512,512]{1,0:T(8,128)(2,1)}, u32[]{:S(2)}) %copy-start.1) | copy-done | bytes 524312
  36.2 17.3 %scatter.1 = bf16[512,512]{1,0:T(8,128)(2,1)S(1)} custom-call(bf16[512,512]{1,0:T(8,128)(2,1)S(1)} %copy-done.1, bf16[512,2048]{1,0:T(8,128)(2,1)S(1)} %copy-done), custom_call_target="tpu_custom_call" | custom-call | tf_op jit(solution)/shard_map/scatter/pallas_call | solution.py:374
  53.5 0.8 %copy.11 = bf16[512,512]{1,0:T(8,128)(2,1)} copy(bf16[512,512]{1,0:T(8,128)(2,1)S(1)} %scatter.1) | data formatting | bytes 1048576
Async XLA Ops:
  5.0 30.2 %copy-start = (bf16[512,2048]{1,0:T(8,128)(2,1)S(1)}, bf16[512,2048]{1,0:T(8,128)(2,1)}, u32[]{:S(2)}) copy-start(bf16[512,2048]{1,0:T(8,128)(2,1)} %w_hbm.1) | copy-start | bytes 6291460
  35.2 1.0 %copy-start.1 = (bf16[512,512]{1,0:T(8,128)(2,1)S(1)}, bf16[512,512]{1,0:T(8,128)(2,1)}, u32[]{:S(2)}) copy-start(bf16[512,512]{1,0:T(8,128)(2,1)} %attend.1.ho_ref) | copy-start | bytes 1572868

commit v2 on v1

--- a/solution.py
+++ b/solution.py
@@ -3,6 +3,7 @@
 
 import jax
 import jax.numpy as jnp
+import numpy as np
 from jax import lax
 from jax.experimental import pallas as pl
 from jax.experimental.pallas import tpu as pltpu
@@ -25,9 +26,10 @@
 
 
 def attend_kernel(
-    n, reach, tok_hbm, ids_ref, wq_hbm, wd_hbm, gain_ref, wk_hbm, wv_hbm, inv_ref, out_ref,
-    tok, wq, wd, wk, wv, ids_r, lat, rop, q_s, k_s, v_s, beg, top, total, acc,
-    load, s_id, r_id, s_key, r_key, s_fwd, r_fwd,
+    n, reach, chunks, tok_hbm, ids_ref, wq_hbm, wd_hbm, gain_ref, wk_hbm, wv_hbm, w_hbm, inv_ref,
+    out_ref, tok, wq, wd, wk, wv, w, ids_r, pe, lat, rop, q_s, k_s, v_s, beg, top, total, acc, ho,
+    far_out, far_in, own_out, own_in, x_out, x_in,
+    load, s_id, r_id, s_key, r_key, s_fwd, r_fwd, s_far, r_far, s_own, r_own, s_x, r_x,
 ):
     rows = tok.shape[0]
     half = rows // 2
@@ -39,6 +41,10 @@
     head = lax.axis_index("head")
     parity = lax.rem(head, 2)
     mate = head + 1 - 2 * parity
+    across = lax.rem(head + 2, 4)
+    far = lax.rem(mate + 2, 4)
+    columns = out_ref.shape[1]
+    depth = rows // chunks
 
     loads = [
         pltpu.make_async_copy(tok_hbm, tok, load.at[0]),
@@ -52,11 +58,15 @@
                 wv_hbm.at[h], wv.at[:, h * value : (h + 1) * value], load.at[4 + h]
             )
         )
-    for copy in loads:
+    for i, target in enumerate((far, across, mate, head)):
+        part = pl.ds(pl.multiple_of(target * columns, columns), columns)
+        loads.append(pltpu.make_async_copy(w_hbm.at[:, part], w.at[i], load.at[4 + heads + i]))
+    for copy in loads[:2]:
         copy.start()
 
     barrier = pltpu.get_barrier_semaphore()
-    pl.semaphore_signal(barrier, inc=1, device_id=(seq, mate), device_id_type=MESH)
+    for other in (mate, across):
+        pl.semaphore_signal(barrier, inc=1, device_id=(seq, other), device_id_type=MESH)
     for d in range(1, reach + 1):
 
         @pl.when(seq + d < n)
@@ -68,7 +78,7 @@
             pl.semaphore_signal(barrier, inc=1, device_id=(seq - d, head), device_id_type=MESH)
 
     pl.semaphore_wait(
-        barrier, 1 + jnp.minimum(seq, reach) + jnp.minimum(n - 1 - seq, reach)
+        barrier, 2 + jnp.minimum(seq, reach) + jnp.minimum(n - 1 - seq, reach)
     )
 
     def id_copy(d):
@@ -112,12 +122,28 @@
 
     loads[0].wait()
     loads[1].wait()
-    down = dot(tok[...], wd[...])
-    raw = down[:, :latent_width]
-    latent = (
-        raw * lax.rsqrt(jnp.mean(raw * raw, axis=1, keepdims=True) + epsilon) * gain_ref[...]
-    )
-    lat[0] = latent.astype(bf16)
+    for copy in loads[2:]:
+        copy.start()
+
+    def project(part):
+        down = dot_t(tok[part], wd[...])
+        raw = down[:, :latent_width]
+        latent = (
+            raw * lax.rsqrt(jnp.mean(raw * raw, axis=1, keepdims=True) + epsilon) * gain_ref[...]
+        )
+        lat[0, part] = latent.astype(bf16)
+        pe[part] = down[:, latent_width:]
+
+    def send_keys(i):
+        for d in range(1, reach + 1):
+
+            @pl.when(seq + d < n)
+            def _():
+                key_copies(d)[i].start()
+
+    project(lat_rows)
+    send_keys(0)
+    project(pl.ds(pl.multiple_of((1 - parity) * half, half), half))
 
     for d in range(1, reach + 1):
 
@@ -143,15 +169,10 @@
         swapped = jnp.concatenate([v[:, rope // 2 :], v[:, : rope // 2]], axis=1)
         return (v * cosine + swapped * sine).astype(bf16)
 
-    key_rope = rotate(down[:, latent_width:])
+    key_rope = rotate(pe[...])
     rop[0] = jnp.concatenate([key_rope[:half], key_rope[half:]], axis=1)
 
-    for d in range(1, reach + 1):
-
-        @pl.when(seq + d < n)
-        def _():
-            for copy in key_copies(d):
-                copy.start()
+    send_keys(1)
 
     loads[2].wait()
     query = dot(tok[...], wq[...]).astype(bf16)
@@ -211,66 +232,9 @@
                 total[mine] = jnp.broadcast_to(sums, (half, 128))
                 acc[mine] = mixed
             else:
-                out_ref[q_at : q_at + half, h * value : (h + 1) * value] = (mixed / sums).astype(
+                ho[q_at : q_at + half, h * value : (h + 1) * value] = (mixed / sums).astype(
                     bf16
                 )
-
-    expand(0)
-    piece(0, 0, 0, half)
-    piece(0, 1, 0, rows)
-    for d in range(1, reach + 1):
-
-        @pl.when(seq >= d)
-        def _():
-            for copy, forward in zip(key_copies(d), forward_copies(d)):
-                copy.wait_recv()
-                forward.start()
-
-    for d in range(1, reach + 1):
-
-        @pl.when(seq >= d)
-        def _():
-            for forward in forward_copies(d):
-                forward.wait_recv()
-
-        expand(d)
-        piece(d, 0, 0, rows)
-        piece(d, 1, half if d == reach else 0, rows)
-
-    for d in range(1, reach + 1):
-
-        @pl.when(seq + d < n)
-        def _():
-            id_copy(d).wait_send()
-            for copy in key_copies(d):
-                copy.wait_send()
-
-        @pl.when(seq >= d)
-        def _():
-            for forward in forward_copies(d):
-                forward.wait_send()
-
-
-def scatter_kernel(
-    chunks, ho_ref, w_hbm, out_ref, w, far_out, far_in, own_out, own_in, x_out, x_in,
-    load, s_far, r_far, s_own, r_own, s_x, r_x,
-):
-    seq = lax.axis_index("seq")
-    head = lax.axis_index("head")
-    columns = out_ref.shape[1]
-    depth = out_ref.shape[0] // chunks
-    mate = head + 1 - 2 * lax.rem(head, 2)
-    across = lax.rem(head + 2, 4)
-    far = lax.rem(mate + 2, 4)
-    loads = []
-    for i, target in enumerate((far, across, mate, head)):
-        part = pl.ds(pl.multiple_of(target * columns, columns), columns)
-        loads.append(pltpu.make_async_copy(w_hbm.at[:, part], w.at[i], load.at[i]))
-        loads[i].start()
-    barrier = pltpu.get_barrier_semaphore()
-    for other in (mate, across):
-        pl.semaphore_signal(barrier, inc=1, device_id=(seq, other), device_id_type=MESH)
-    pl.semaphore_wait(barrier, 2)
 
     def send(src, dst, c, s, r, other):
         return pltpu.make_async_remote_copy(
@@ -278,27 +242,52 @@
             device_id=(seq, other), device_id_type=MESH,
         )
 
-    def partial(c, i):
-        return dot(ho_ref[c * depth : (c + 1) * depth], w[i])
-
     to_far = [send(far_out, far_in, c, s_far, r_far, mate) for c in range(chunks)]
     to_own = [send(own_out, own_in, c, s_own, r_own, mate) for c in range(chunks)]
     to_x = [send(x_out, x_in, c, s_x, r_x, across) for c in range(chunks)]
-    loads[0].wait()
-    for c in range(chunks):
-        far_out[c] = partial(c, 0).astype(bf16)
-        to_far[c].start()
-    loads[1].wait()
-    for c in range(chunks):
-        mine = partial(c, 1)
-        to_far[c].wait_recv()
-        x_out[c] = (mine + far_in[c].astype(f32)).astype(bf16)
-        to_x[c].start()
-    loads[2].wait()
+
+    def partial(c, i):
+        return dot(ho[c * depth : (c + 1) * depth], w[i])
+
+    def reduce_far(part):
+        mine = range(part * chunks // 2, (part + 1) * chunks // 2)
+        for c in mine:
+            far_out[c] = partial(c, 0).astype(bf16)
+            to_far[c].start()
+        for c in mine:
+            ours = partial(c, 1)
+            to_far[c].wait_recv()
+            x_out[c] = (ours + far_in[c].astype(f32)).astype(bf16)
+            to_x[c].start()
+
+    expand(0)
+    piece(0, 0, 0, half)
+    piece(0, 1, 0, rows)
+    for d in range(1, reach + 1):
+
+        @pl.when(seq >= d)
+        def _():
+            for copy, forward in zip(key_copies(d), forward_copies(d)):
+                copy.wait_recv()
+                forward.start()
+
+    for d in range(1, reach + 1):
+
+        @pl.when(seq >= d)
+        def _():
+            for forward in forward_copies(d):
+                forward.wait_recv()
+
+        expand(d)
+        piece(d, 0, 0, rows)
+        if d == reach:
+            reduce_far(0)
+        piece(d, 1, half if d == reach else 0, rows)
+
+    reduce_far(1)
     for c in range(chunks):
         own_out[c] = partial(c, 2).astype(bf16)
         to_own[c].start()
-    loads[3].wait()
     for c in range(chunks):
         mine = partial(c, 3)
         to_own[c].wait_recv()
@@ -308,6 +297,19 @@
     for copy in to_far + to_own + to_x:
         copy.wait_send()
 
+    for d in range(1, reach + 1):
+
+        @pl.when(seq + d < n)
+        def _():
+            id_copy(d).wait_send()
+            for copy in key_copies(d):
+                copy.wait_send()
+
+        @pl.when(seq >= d)
+        def _():
+            for forward in forward_copies(d):
+                forward.wait_send()
+
 
 def local(tokens, seq_ids, w_query, w_down, latent_gain, w_key_up, w_value_up, w_out):
     rows, width = tokens.shape
@@ -317,23 +319,30 @@
     n = lax.axis_size("seq")
     groups = lax.axis_size("head")
     reach = max(1, n // 4)
+    chunks = 4
+    columns = w_out.shape[1] // groups
+    block = (chunks, rows // chunks, columns)
     padded = -(-(nope + rope) // 128) * 128
-    inverse = 10000.0 ** (-2.0 * jnp.arange(rope // 2, dtype=f32) / rope)
+    inverse = np.float32(10000.0) ** (
+        np.float32(-2.0) * np.arange(rope // 2, dtype=np.float32) / np.float32(rope)
+    )
     vmem = pl.BlockSpec(memory_space=pltpu.VMEM)
     anywhere = pl.BlockSpec(memory_space=pl.ANY)
     dma = pltpu.SemaphoreType.DMA
-    head_out = pl.pallas_call(
-        functools.partial(attend_kernel, n, reach),
-        out_shape=jax.ShapeDtypeStruct((rows, heads * value), bf16),
-        in_specs=[anywhere, vmem, anywhere, anywhere, vmem, anywhere, anywhere, vmem],
+    return pl.pallas_call(
+        functools.partial(attend_kernel, n, reach, chunks),
+        out_shape=jax.ShapeDtypeStruct((rows, columns), bf16),
+        in_specs=[anywhere, vmem, anywhere, anywhere, vmem, anywhere, anywhere, anywhere, vmem],
         out_specs=vmem,
         scratch_shapes=[
             pltpu.VMEM((rows, width), bf16),
             pltpu.VMEM(w_query.shape, bf16),
-            pltpu.VMEM(w_down.shape, bf16),
+            pltpu.VMEM(w_down.shape[::-1], bf16),
             pltpu.VMEM((heads * nope, latent_width), bf16),
             pltpu.VMEM((latent_width, heads * value), bf16),
+            pltpu.VMEM((groups, w_out.shape[0], columns), bf16),
             pltpu.VMEM((reach, 1, rows), jnp.int32),
+            pltpu.VMEM((rows, rope), f32),
             pltpu.VMEM((reach + 1, rows, latent_width), bf16),
             pltpu.VMEM((reach + 1, rows // 2, 2 * rope), bf16),
             pltpu.VMEM((heads, rows, padded), bf16),
@@ -343,14 +352,19 @@
             pltpu.VMEM((heads, rows, 128), f32),
             pltpu.VMEM((heads, rows, 128), f32),
             pltpu.VMEM((heads, rows, value), f32),
-            dma((4 + heads,)),
+            pltpu.VMEM((rows, heads * value), bf16),
+        ]
+        + [pltpu.VMEM(block, bf16)] * 6
+        + [
+            dma((4 + heads + groups,)),
             dma((reach,)),
             dma((reach,)),
             dma((reach, 2)),
             dma((reach, 2)),
             dma((reach, 2)),
             dma((reach, 2)),
-        ],
+        ]
+        + [dma((chunks,))] * 6,
         compiler_params=pltpu.CompilerParams(
             collective_id=0, has_side_effects=True, vmem_limit_bytes=56 * 1024 * 1024
         ),
@@ -359,32 +373,13 @@
         tokens,
         seq_ids.reshape(1, rows),
         w_query,
-        w_down,
+        w_down.T,
         latent_gain.reshape(1, latent_width),
         w_key_up.reshape(heads * nope, latent_width),
         w_value_up,
-        inverse.reshape(rope // 2, 1),
+        w_out,
+        jnp.asarray(inverse.reshape(rope // 2, 1)),
     )
-    columns = w_out.shape[1] // groups
-    if groups != 4:
-        partial = dot(head_out, w_out).astype(bf16)
-        return lax.psum_scatter(partial, "head", scatter_dimension=1, tiled=True)
-    chunks = 4
-    block = (chunks, rows // chunks, columns)
-    return pl.pallas_call(
-        functools.partial(scatter_kernel, chunks),
-        out_shape=jax.ShapeDtypeStruct((rows, columns), bf16),
-        in_specs=[vmem, anywhere],
-        out_specs=vmem,
-        scratch_shapes=[pltpu.VMEM((4, w_out.shape[0], columns), bf16)]
-        + [pltpu.VMEM(block, bf16)] * 6
-        + [dma((4,))]
-        + [dma((chunks,))] * 6,
-        compiler_params=pltpu.CompilerParams(
-            collective_id=1, has_side_effects=True, vmem_limit_bytes=32 * 1024 * 1024
-        ),
-        name="scatter",
-    )(head_out, w_out)
 
 
 def solution(mesh):

time: 54.6 us -> 44.1 us (0.81)
  the two profiles are of different devices: /device:TPU:23 before, /device:TPU:8 now
where the time goes in v2:
time: 44.1 us; the launch traced here: 43.9 us
  Pallas kernels  42 us (95%)
  local copies, waits for them, and re-layouts  1.87 us (4%)
    pallas_call x1, Pallas kernels, local(): pl.pallas_call(functools.partial(attend_kernel, n, reach, chunks), out_sh...  42 us
    unnamed x1, local copies, waits for them, and re-layouts  1.87 us

profile of v2, /device:TPU:8, one launch (start us, length us, event | category | flops | bytes accessed | tf_op | source)
XLA Modules:
  0.0 43.9 jit_solution(9154062628401754108)
XLA Ops:
  0.0 42.0 %attend.1 = bf16[512,512]{1,0:T(8,128)(2,1)} custom-call(bf16[512,2048]{1,0:T(8,128)(2,1)} %tok_hbm.1, s32[1,512]{1,0:T(1,128)} %bitcast.6, bf16[2048,768]{1,0:T(8,128)(2,1)} %wq_hbm.1, bf16[576,2048]{1,0:T(8,128)(2,1)} %bitcast.4, f32[1,512]{1,0:T(1,128)} %bitcast.7, bf16[512,512]{1,0:T(8,128)(2,1)} %bitcast.5, bf16[4,512,128]{2,1,0:T(8,128)(2,1)} %wv_hbm.1, ...), custom_call_target="tpu_custom_call" | custom-call | tf_op jit(solution)/shard_map/attend/pallas_call | solution.py:332
  42.0 1.9 %copy.11 = bf16[512,512]{1,0:T(8,128)(2,1)} copy(bf16[512,512]{1,0:T(8,128)(2,1)} %attend.1) | data formatting | bytes 1048576

commit v3 on v2

--- a/solution.py
+++ b/solution.py
@@ -260,17 +260,17 @@
             x_out[c] = (ours + far_in[c].astype(f32)).astype(bf16)
             to_x[c].start()
 
-    expand(0)
-    piece(0, 0, 0, half)
-    piece(0, 1, 0, rows)
-    for d in range(1, reach + 1):
-
+    def pass_on(d):
         @pl.when(seq >= d)
         def _():
             for copy, forward in zip(key_copies(d), forward_copies(d)):
                 copy.wait_recv()
                 forward.start()
 
+    expand(0)
+    piece(0, 0, 0, half)
+    pass_on(1)
+    piece(0, 1, 0, rows)
     for d in range(1, reach + 1):
 
         @pl.when(seq >= d)
@@ -282,6 +282,8 @@
         piece(d, 0, 0, rows)
         if d == reach:
             reduce_far(0)
+        else:
+            pass_on(d + 1)
         piece(d, 1, half if d == reach else 0, rows)
 
     reduce_far(1)

time: 44.1 us -> 45.8 us (1.039)
  Pallas kernels: 42 us -> 43.4 us
    pallas_call x1, Pallas kernels: 42 us -> 43.4 us  [local(): pl.pallas_call(functools.partial(attend_kernel, n, reach, chunks), out_sh...]
where the time goes in v3:
time: 45.8 us; the launch traced here: 45.3 us
  Pallas kernels  43.4 us (95%)
  local copies, waits for them, and re-layouts  1.87 us (4%)
    pallas_call x1, Pallas kernels, local(): pl.pallas_call(functools.partial(attend_kernel, n, reach, chunks), out_sh...  43.4 us
    unnamed x1, local copies, waits for them, and re-layouts  1.87 us

profile of v3, /device:TPU:8, one launch (start us, length us, event | category | flops | bytes accessed | tf_op | source)
XLA Modules:
  0.0 45.3 jit_solution(1103538303170958850)
XLA Ops:
  0.0 43.4 %attend.1 = bf16[512,512]{1,0:T(8,128)(2,1)} custom-call(bf16[512,2048]{1,0:T(8,128)(2,1)} %tok_hbm.1, s32[1,512]{1,0:T(1,128)} %bitcast.6, bf16[2048,768]{1,0:T(8,128)(2,1)} %wq_hbm.1, bf16[576,2048]{1,0:T(8,128)(2,1)} %bitcast.4, f32[1,512]{1,0:T(1,128)} %bitcast.7, bf16[512,512]{1,0:T(8,128)(2,1)} %bitcast.5, bf16[4,512,128]{2,1,0:T(8,128)(2,1)} %wv_hbm.1, ...), custom_call_target="tpu_custom_call" | custom-call | tf_op jit(solution)/shard_map/attend/pallas_call | solution.py:334
  43.4 1.9 %copy.11 = bf16[512,512]{1,0:T(8,128)(2,1)} copy(bf16[512,512]{1,0:T(8,128)(2,1)} %attend.1) | data formatting | bytes 1048576
